TPU v7x, 32 devices: a whole 2x2x4 slice. The times are simulated.
32 devices in a mesh: layer: 4 (over z), row: 2 (over core), col: 4 (over y, x).
Axes of the slice: x: 2, y: 2, z: 4, core: 2. Of those that a mesh axis runs over, the one named last changes fastest.
Arguments:
- panels: float32 [4096, 8192], P('row', ('layer', 'col')), may hold values from -0.0625 to 0.0625
- eigvecs: float32 [8192, 2048], P(('layer', 'row'), 'col'), may hold values from -6 to 6
Outputs:
- result: float32 [4096, 2048], P('row', 'col')
All inputs are finite; a program needn't handle non-finite values.
Results may differ from a plain program's by a relative error of at most 0.0001.
Values sent between devices are 32-bit elements; how exact they have to be, the bound alone decides.
No kernel may reach another device: no remote copies, remote signals or barrier semaphores. Data moves between devices by JAX's collectives and lax.ppermute only.
A program may use at most 64 MiB of HBM per device.

v0:
```python
import jax
import jax.numpy as jnp
from jax import lax
from jax.sharding import PartitionSpec as P


def local(panels, eigvecs):
    layer_vecs = lax.all_gather(eigvecs, "row", axis=0, tiled=True)
    partial_sum = jnp.dot(
        lax.all_gather(panels, "col", axis=1, tiled=True),
        layer_vecs,
        preferred_element_type=jnp.float32,
        precision=lax.Precision.HIGHEST,
    )
    result = lax.psum(partial_sum, "layer")
    return result


def solution(mesh):
    in_specs = (P("row", ("layer", "col")), P(("layer", "row"), "col"))
    out_specs = P("row", "col")
    return jax.shard_map(local, mesh=mesh, in_specs=in_specs, out_specs=out_specs, check_vma=False)
```

profile of v0, /device:TPU:0, one launch (start us, length us, event | category | flops | bytes accessed | tf_op | source)
XLA Modules:
  0.0 383.9 jit_solution(4425001586556484213)
XLA Ops:
  6.5 0.0 all-gather.5.cloned.1.call-start
  6.5 0.7 all-gather.5.cloned.1.call-update
  7.3 0.0 all-gather.3.cloned.1.call-start
  7.3 0.7 all-gather.3.cloned.1.call-update
  8.0 0.0 all-reduce.2.cloned.1.call-start
  8.1 17.2 %all-gather.5.cloned.1.call-done = f32[2048,512]{1,0:T(8,128)} async-done(((f32[1024,512]{1,0:T(8,128)}), f32[2048,512]{1,0:T(8,128)}) %all-gather.5.cloned.1.call-update) | async-done | bytes 4194320 | tf_op jit(solution)/shard_map/all_gather | solution.py:8
  25.3 160.3 %all-gather.3.cloned.1.call-done = f32[2048,2048]{1,0:T(8,128)} async-done(((f32[2048,512]{1,0:T(8,128)}), f32[2048,2048]{1,0:T(8,128)}) %all-gather.3.cloned.1.call-update) | async-done | bytes 16777232 | tf_op jit(solution)/shard_map/all_gather | solution.py:10
  185.6 31.9 %fusion = f32[2048,512]{1,0:T(8,128)} fusion(f32[2048,2048]{1,0:T(8,128)} %all-gather.3.cloned.1.call-done, f32[2048,512]{1,0:T(8,128)} %all-gather.5.cloned.1.call-done), kind=kOutput, calls=%fused_computation | convolution fusion | flops 25769803776 | bytes 25165824 | tf_op jit(solution)/shard_map/dot_general | solution.py:9
  217.6 0.0 all-reduce.2.cloned.1.call-update
  217.6 155.1 %all-reduce.2.cloned.1.call-done = f32[2048,512]{1,0:T(8,128)} async-done(((f32[2048,512]{1,0:T(8,128)}), f32[2048,512]{1,0:T(8,128)}) %all-reduce.2.cloned.1.call-update) | async-done | bytes 4194320 | tf_op jit(solution)/shard_map/psum | solution.py:15
  372.7 4.6 %copy.4 = f32[2048,512]{1,0:T(8,128)} copy(f32[2048,512]{1,0:T(8,128)} %all-reduce.2.cloned.1.call-done) | data formatting | bytes 8388608
Async XLA Ops:
  6.5 18.8 %all-gather.5.cloned.1.call-start = ((), (), s32[]{:S(2)}) async-start(), calls=%async_computation.1 | async-start | bytes 6291456 | tf_op jit(solution)/shard_map/all_gather | solution.py:8
  7.3 178.4 %all-gather.3.cloned.1.call-start = ((), (), s32[]{:S(2)}) async-start(), calls=%async_computation | async-start | bytes 20971520 | tf_op jit(solution)/shard_map/all_gather | solution.py:10
  8.0 364.7 %all-reduce.2.cloned.1.call-start = ((), (), s32[]{:S(2)}) async-start(), calls=%async_computation.2 | async-start | bytes 8388608 | tf_op jit(solution)/shard_map/psum | solution.py:15
Sparse Core Ops, SparseCore 0:
  8.9 16.3 all-gather.4
  27.1 158.4 all-gather.2
  217.7 154.9 all-reduce.1
where the time goes:
time: 384 us
  waiting for transfers between devices  334 us (87%)
  matrix products  31.9 us (8%)
  between operations  13.1 us (3%)
  local copies, waits for them, and re-layouts  4.64 us (1%)
    all_gather x1, waiting for transfers between devices, local(): lax.all_gather(panels, 'col', axis=1, tiled=True)  160 us
    psum x1, waiting for transfers between devices, local(): result = lax.psum(partial_sum, 'layer')  155 us
    dot_general x1, matrix products, local(): jnp.dot(lax.all_gather(panels, 'col', axis=1, tiled=True), layer_vecs, pr...  31.9 us
    all_gather x1, waiting for transfers between devices, local(): layer_vecs = lax.all_gather(eigvecs, 'row', axis=0, tiled=True)  17.2 us
  transfers between devices with their start and end apart: 3, of which 3 were waited for; matrix products, arithmetic and copies ran while one was open for 0% of the time, Pallas kernels for 0%

commit v1 on v0

--- a/solution.py
+++ b/solution.py
@@ -12,7 +12,7 @@
         preferred_element_type=jnp.float32,
         precision=lax.Precision.HIGHEST,
     )
-    result = lax.psum(partial_sum, "layer")
+    result = jnp.sum(lax.all_gather(partial_sum, "layer"), 0)
     return result
 
 

time: 384 us -> 522 us (1.36)
  waiting for transfers between devices: 334 us -> 466 us
  other arithmetic: 0 us -> 10.4 us
    all_gather x0 -> x1, waiting for transfers between devices: none -> 287 us  [local(): result = jnp.sum(lax.all_gather(partial_sum, 'layer'), 0)]
    psum x1 -> x0, waiting for transfers between devices: 155 us -> none  [local(): result = lax.psum(partial_sum, 'layer')]
    reduce_sum x0 -> x1, other arithmetic: none -> 10.4 us  [local(): result = jnp.sum(lax.all_gather(partial_sum, 'layer'), 0)]
where the time goes in v1:
time: 522 us; the launch traced here: 521 us
  waiting for transfers between devices  466 us (89%)
  matrix products  31.9 us (6%)
  between operations  13.1 us (3%)
  other arithmetic  10.4 us (2%)
    all_gather x1, waiting for transfers between devices, local(): result = jnp.sum(lax.all_gather(partial_sum, 'layer'), 0)  287 us
    all_gather x1, waiting for transfers between devices, local(): lax.all_gather(panels, 'col', axis=1, tiled=True)  160 us
    dot_general x1, matrix products, local(): jnp.dot(lax.all_gather(panels, 'col', axis=1, tiled=True), layer_vecs, pr...  31.9 us
    all_gather x1, waiting for transfers between devices, local(): layer_vecs = lax.all_gather(eigvecs, 'row', axis=0, tiled=True)  17.2 us
  transfers between devices with their start and end apart: 3, of which 3 were waited for; matrix products, arithmetic and copies ran while one was open for 0% of the time, Pallas kernels for 0%

profile of v1, /device:TPU:0, one launch (start us, length us, event | category | flops | bytes accessed | tf_op | source)
XLA Modules:
  0.0 521.4 jit_solution(11673238801513990992)
XLA Ops:
  6.5 0.0 all-gather.7.cloned.1.call-start
  6.5 0.7 all-gather.7.cloned.1.call-update
  7.3 0.0 all-gather.5.cloned.1.call-start
  7.3 0.7 all-gather.5.cloned.1.call-update
  8.0 0.0 all-gather.9.cloned.1.call-start
  8.1 17.2 %all-gather.7.cloned.1.call-done = f32[2048,512]{1,0:T(8,128)} async-done(((f32[1024,512]{1,0:T(8,128)}), f32[2048,512]{1,0:T(8,128)}) %all-gather.7.cloned.1.call-update) | async-done | bytes 4194320 | tf_op jit(solution)/shard_map/all_gather | solution.py:8
  25.3 160.3 %all-gather.5.cloned.1.call-done = f32[2048,2048]{1,0:T(8,128)} async-done(((f32[2048,512]{1,0:T(8,128)}), f32[2048,2048]{1,0:T(8,128)}) %all-gather.5.cloned.1.call-update) | async-done | bytes 16777232 | tf_op jit(solution)/shard_map/all_gather | solution.py:10
  185.6 31.9 %fusion = f32[2048,512]{1,0:T(8,128)} fusion(f32[2048,2048]{1,0:T(8,128)} %all-gather.5.cloned.1.call-done, f32[2048,512]{1,0:T(8,128)} %all-gather.7.cloned.1.call-done), kind=kOutput, calls=%fused_computation | convolution fusion | flops 25769803776 | bytes 25165824 | tf_op jit(solution)/shard_map/dot_general | solution.py:9
  217.6 0.0 all-gather.9.cloned.1.call-update
  217.6 286.9 %all-gather.9.cloned.1.call-done = f32[8192,512]{1,0:T(8,128)} async-done(((f32[2048,512]{1,0:T(8,128)}), f32[8192,512]{1,0:T(8,128)}) %all-gather.9.cloned.1.call-update) | async-done | bytes 16777232 | tf_op jit(solution)/shard_map/all_gather | solution.py:15
  504.5 10.4 %reduce_sum.9 = f32[2048,512]{1,0:T(8,128)} reduce(f32[4,2048,512]{2,1,0:T(8,128)} %bitcast.3, f32[]{:T(128)} %constant.0.clone.1), dimensions={0}, to_apply=%region_0.0 | reduce | flops 3145728 | bytes 20971524 | tf_op jit(solution)/shard_map/reduce_sum | solution.py:15
Async XLA Ops:
  6.5 18.8 %all-gather.7.cloned.1.call-start = ((), (), s32[]{:S(2)}) async-start(), calls=%async_computation.1 | async-start | bytes 6291456 | tf_op jit(solution)/shard_map/all_gather | solution.py:8
  7.3 178.4 %all-gather.5.cloned.1.call-start = ((), (), s32[]{:S(2)}) async-start(), calls=%async_computation | async-start | bytes 20971520 | tf_op jit(solution)/shard_map/all_gather | solution.py:10
  8.0 496.5 %all-gather.9.cloned.1.call-start = ((), (), s32[]{:S(2)}) async-start(), calls=%async_computation.2 | async-start | bytes 20971520 | tf_op jit(solution)/shard_map/all_gather | solution.py:15
Sparse Core Ops, SparseCore 0:
  8.9 16.3 all-gather.6
  27.1 158.4 all-gather.4
  217.7 286.7 all-gather.8
